TPU v7x, 32 devices: a whole 2x2x4 slice. The times are simulated.
32 devices in a mesh: gx: 8 (over z, x), gy: 4 (over y, core).
Axes of the slice: x: 2, y: 2, z: 4, core: 2. Of those that a mesh axis runs over, the one named last changes fastest.
Arguments:
- field: float32 [128, 64, 128], P('gx', 'gy'), may hold values from -6 to 6
- conductance: float32 [128, 64, 128], P('gx', 'gy'), may hold values from 200 to 5000
- source: float32 [128, 64, 128], P('gx', 'gy'), may hold values from -600 to 600
Outputs:
- advanced: float32 [128, 64, 128], P('gx', 'gy')
All inputs are finite; a program needn't handle non-finite values.
Results may differ from a plain program's by a relative error of at most 0.0003.
Values sent between devices are 32-bit elements; how exact they have to be, the bound alone decides.
A program may use at most 64 MiB of HBM per device.

v0:
```python
import jax
import jax.numpy as jnp
from jax import lax
from jax.sharding import PartitionSpec as P


def padded_2(cells, sides, width):
    for axis, dim in sides:
        count = lax.axis_size(axis)
        ends = count - 1
        head = lax.slice_in_dim(cells, 0, width, axis=dim)
        tail = lax.slice_in_dim(cells, cells.shape[dim] - width, cells.shape[dim], axis=dim)
        cells = jnp.concatenate(
            [
                lax.ppermute(tail, axis, [(i, (i + 1) % count) for i in range(ends)]),
                cells,
                lax.ppermute(head, axis, [((i + 1) % count, i) for i in range(ends)]),
            ],
            axis=dim,
        )
    return cells


def thomas(lower, diag, upper, rights):
    stacked = jnp.stack(rights, axis=1)

    def forward_step(carry, items):
        prev_ratio, prev_value = carry
        low, dia, upp, rig = items
        pivot = dia - low * prev_ratio
        inverse = 1.0 / pivot
        ratio = upp * inverse
        value = (rig - low[None] * prev_value) * inverse[None]
        return ((ratio, value), (ratio, value))

    start = (jnp.zeros_like(diag[0]), jnp.zeros_like(stacked[0]))
    unused, (ratios, values) = lax.scan(forward_step, start, (lower, diag, upper, stacked))

    def backward_step(following, items):
        ratio, value = items
        solved = value - ratio[None] * following
        return (solved, solved)

    unused_back, solved = lax.scan(
        backward_step, jnp.zeros_like(stacked[0]), (ratios, values), reverse=True
    )
    return [solved[:, j] for j in range(len(rights))]


def join(left, right):
    pfa, afa, bfa, pla, ala, bla = left
    pfb, afb, bfb, plb, alb, blb = right
    scale = 1.0 / (1.0 - bla * afb)
    mid_p = (pla + bla * pfb) * scale
    mid_a = ala * scale
    mid_b = bla * bfb * scale
    next_p = pfb + afb * mid_p
    next_a = afb * mid_a
    next_b = bfb + afb * mid_b
    return (
        pfa + bfa * next_p,
        afa + bfa * next_a,
        bfa * next_b,
        plb + alb * mid_p,
        alb * mid_a,
        blb + alb * mid_b,
    )


def neutral(sample):
    zeros = jnp.zeros_like(sample)
    ones = jnp.ones_like(sample)
    return (zeros, zeros, ones, zeros, ones, zeros)


def sweep_table(table, position):
    count = table[0].shape[0]
    start = neutral(table[0][0])

    def step(k, carry):
        before, after = carry
        piece = tuple((item[k] for item in table))
        joined = join(before, piece)
        before = tuple((jnp.where(k < position, new, old) for new, old in zip(joined, before)))
        back = count - 1 - k
        piece = tuple((item[back] for item in table))
        joined = join(piece, after)
        after = tuple((jnp.where(back > position, new, old) for new, old in zip(joined, after)))
        return (before, after)

    return lax.fori_loop(0, count, step, (start, start))


def partitioned(lower, diag, upper, right, couple):
    length = diag.shape[0]
    inner = right[1:-1]
    zeros = jnp.zeros_like(inner)
    from_first = zeros.at[0].set(-lower[1])
    from_last = zeros.at[-1].set(-upper[length - 2])
    base, first_part, last_part = thomas(
        lower[1:-1], diag[1:-1], upper[1:-1], [inner, from_first, from_last]
    )
    top_a = diag[0] + upper[0] * first_part[0]
    top_b = upper[0] * last_part[0]
    top_r = right[0] - upper[0] * base[0]
    bot_a = lower[length - 1] * first_part[-1]
    bot_b = diag[length - 1] + lower[length - 1] * last_part[-1]
    bot_r = right[length - 1] - lower[length - 1] * base[-1]
    inverse = 1.0 / (top_a * bot_b - top_b * bot_a)
    edge_lo = lower[0]
    edge_hi = upper[length - 1]
    coeffs = (
        (bot_b * top_r - top_b * bot_r) * inverse,
        -bot_b * edge_lo * inverse,
        top_b * edge_hi * inverse,
        (top_a * bot_r - bot_a * top_r) * inverse,
        bot_a * edge_lo * inverse,
        -top_a * edge_hi * inverse,
    )
    before, after = couple(coeffs)
    pfo, afo, bfo, plo, alo, blo = coeffs
    prev_p, prev_b = (before[3], before[5])
    next_p, next_a = (after[0], after[1])
    m_ff = 1.0 - afo * prev_b
    m_fl = -bfo * next_a
    m_lf = -alo * prev_b
    m_ll = 1.0 - blo * next_a
    r_f = pfo + afo * prev_p + bfo * next_p
    r_l = plo + alo * prev_p + blo * next_p
    inverse = 1.0 / (m_ff * m_ll - m_fl * m_lf)
    first_val = (m_ll * r_f - m_fl * r_l) * inverse
    last_val = (m_ff * r_l - m_lf * r_f) * inverse
    middle = base + first_part * first_val + last_part * last_val
    return jnp.concatenate([first_val[None], middle, last_val[None]], axis=0)


def body(field, conductance, source):
    stacked = jnp.stack([field, conductance])
    padded = padded_2(stacked, (("gx", 1), ("gy", 2)), 1)
    nearby = padded[0]
    cond = padded[1]
    faces_x = 0.5 * (cond[:-1, 1:-1] + cond[1:, 1:-1])
    faces_y = 0.5 * (cond[1:-1, :-1] + cond[1:-1, 1:])
    cond_z = jnp.pad(conductance, ((0, 0), (0, 0), (1, 1)))
    faces_z = 0.5 * (cond_z[..., :-1] + cond_z[..., 1:])
    flux_x = faces_x * (nearby[1:, 1:-1] - nearby[:-1, 1:-1])
    apply_x = flux_x[1:] - flux_x[:-1]
    flux_y = faces_y * (nearby[1:-1, 1:] - nearby[1:-1, :-1])
    apply_y = flux_y[:, 1:] - flux_y[:, :-1]
    field_z = jnp.pad(field, ((0, 0), (0, 0), (1, 1)))
    flux_z = faces_z * (field_z[..., 1:] - field_z[..., :-1])
    apply_z = flux_z[..., 1:] - flux_z[..., :-1]
    first = field + 0.5 * apply_x + apply_y + apply_z + source

    def couple_x(coeffs):
        table = (
            lax.all_gather(coeffs[0][None], "gx", axis=0, tiled=True),
            lax.all_gather(coeffs[1][None], "gx", axis=0, tiled=True),
            lax.all_gather(coeffs[2][None], "gx", axis=0, tiled=True),
            lax.all_gather(coeffs[3][None], "gx", axis=0, tiled=True),
            lax.all_gather(coeffs[4][None], "gx", axis=0, tiled=True),
            lax.all_gather(coeffs[5][None], "gx", axis=0, tiled=True),
        )
        return sweep_table(table, lax.axis_index("gx"))

    def couple_y(coeffs):
        table = (
            lax.all_gather(coeffs[0][None], "gy", axis=0, tiled=True),
            lax.all_gather(coeffs[1][None], "gy", axis=0, tiled=True),
            lax.all_gather(coeffs[2][None], "gy", axis=0, tiled=True),
            lax.all_gather(coeffs[3][None], "gy", axis=0, tiled=True),
            lax.all_gather(coeffs[4][None], "gy", axis=0, tiled=True),
            lax.all_gather(coeffs[5][None], "gy", axis=0, tiled=True),
        )
        return sweep_table(table, lax.axis_index("gy"))

    lower_x = -0.5 * faces_x[:-1]
    upper_x = -0.5 * faces_x[1:]
    section_x = partitioned(lower_x, 1.0 - lower_x - upper_x, upper_x, first, couple_x)
    moved_faces = jnp.moveaxis(faces_y, 1, 0)
    lower_y = -0.5 * moved_faces[:-1]
    upper_y = -0.5 * moved_faces[1:]
    second = jnp.moveaxis(section_x - 0.5 * apply_y, 1, 0)
    section_y = jnp.moveaxis(
        partitioned(lower_y, 1.0 - lower_y - upper_y, upper_y, second, couple_y), 0, 1
    )
    rows_x, rows_y, depth = field.shape
    third = jnp.moveaxis(section_y - 0.5 * apply_z, 2, 0).reshape(depth, rows_x * rows_y)
    flat_faces = jnp.moveaxis(faces_z, 2, 0).reshape(depth + 1, rows_x * rows_y)
    lower_z = -0.5 * flat_faces[:-1]
    upper_z = -0.5 * flat_faces[1:]
    solved = thomas(lower_z, 1.0 - lower_z - upper_z, upper_z, [third])[0]
    return jnp.moveaxis(solved.reshape(depth, rows_x, rows_y), 0, 2)


def solution(mesh):
    return jax.shard_map(
        body,
        mesh=mesh,
        in_specs=(P("gx", "gy", None), P("gx", "gy", None), P("gx", "gy", None)),
        out_specs=P("gx", "gy", None),
        check_vma=False,
    )
```

profile of v0, /device:TPU:0, one launch (start us, length us, event | category | flops | bytes accessed | tf_op | source)
XLA Modules:
  0.0 264.4 jit_solution(9152851236280427490)
XLA Ops:
  0.0 1.0 copy_bitcast_fusion
  1.1 5.0 %collective-permute-start = (f32[2,1,16,128]{3,1,2,0:T(1,128)S(1)}, f32[2,1,16,128]{3,1,2,0:T(1,128)S(1)}, u32[]{:S(2)}, u32[]{:S(2)}) collective-permute-start(f32[2,1,16,128]{3,1,2,0:T(1,128)S(1)} %get-tuple-element.1588), channel_id=1, source_target_pairs={{0,4},{4,8},{8,12},{12,16},{16,20},{20,24},{24,28},{1,5},{5,9},{9,... | collective-permute-start | bytes 49160 | tf_op jit(solution)/shard_map/ppermute | solution.py:15
  6.1 1.3 collective-permute-start.1
  7.9 3.9 %collective-permute-done.1 = f32[2,1,16,128]{3,1,2,0:T(1,128)S(1)} collective-permute-done((f32[2,1,16,128]{3,1,2,0:T(1,128)S(1)}, f32[2,1,16,128]{3,1,2,0:T(1,128)S(1)}, u32[]{:S(2)}, u32[]{:S(2)}) %collective-permute-start.1) | collective-permute-done | bytes 16416 | tf_op jit(solution)/shard_map/ppermute | solution.py:17
  11.8 1.3 collective-permute-start.2
  13.1 1.3 collective-permute-start.3
  15.0 2.9 %collective-permute-done.3 = f32[2,18,1,128]{3,1,2,0:T(8,128)S(1)} collective-permute-done((f32[2,18,1,128]{3,1,2,0:T(8,128)S(1)}, f32[2,18,1,128]{3,1,2,0:T(8,128)S(1)}, u32[]{:S(2)}, u32[]{:S(2)}) %collective-permute-start.3) | collective-permute-done | bytes 18464 | tf_op jit(solution)/shard_map/ppermute | solution.py:17
  19.4 0.9 while.150
  20.3 0.8 while.151
  21.4 30.9 %all_gather.37 = f32[8,16,128]{2,1,0:T(8,128)S(1)} all-gather(f32[1,16,128]{2,1,0:T(8,128)S(1)} %multiply_multiply_fusion.7), channel_id=1, replica_groups=mesh['gx'=8,'gy'=4] {'gx'}, dimensions={0}, use_global_device_ids=true | all-gather | bytes 73728 | tf_op jit(solution)/shard_map/all_gather | solution.py:161
  52.3 30.5 %all_gather.36 = f32[8,16,128]{2,1,0:T(8,128)S(1)} all-gather(f32[1,16,128]{2,1,0:T(8,128)S(1)} %get-tuple-element.1583), channel_id=1, replica_groups=mesh['gx'=8,'gy'=4] {'gx'}, dimensions={0}, use_global_device_ids=true | all-gather | bytes 73728 | tf_op jit(solution)/shard_map/all_gather | solution.py:160
  82.9 30.5 %all_gather.38 = f32[8,16,128]{2,1,0:T(8,128)S(1)} all-gather(f32[1,16,128]{2,1,0:T(8,128)S(1)} %get-tuple-element.1582), channel_id=1, replica_groups=mesh['gx'=8,'gy'=4] {'gx'}, dimensions={0}, use_global_device_ids=true | all-gather | bytes 73728 | tf_op jit(solution)/shard_map/all_gather | solution.py:157
  113.4 30.5 %all_gather.39 = f32[8,16,128]{2,1,0:T(8,128)S(1)} all-gather(f32[1,16,128]{2,1,0:T(8,128)S(1)} %get-tuple-element.1599), channel_id=1, replica_groups=mesh['gx'=8,'gy'=4] {'gx'}, dimensions={0}, use_global_device_ids=true | all-gather | bytes 73728 | tf_op jit(solution)/shard_map/all_gather | solution.py:158
  143.9 30.5 %all_gather.40 = f32[8,16,128]{2,1,0:T(8,128)S(1)} all-gather(f32[1,16,128]{2,1,0:T(8,128)S(1)} %get-tuple-element.1596), channel_id=1, replica_groups=mesh['gx'=8,'gy'=4] {'gx'}, dimensions={0}, use_global_device_ids=true | all-gather | bytes 73728 | tf_op jit(solution)/shard_map/all_gather | solution.py:162
  174.4 30.5 %all_gather.41 = f32[8,16,128]{2,1,0:T(8,128)S(1)} all-gather(f32[1,16,128]{2,1,0:T(8,128)S(1)} %get-tuple-element.1562), channel_id=1, replica_groups=mesh['gx'=8,'gy'=4] {'gx'}, dimensions={0}, use_global_device_ids=true | all-gather | bytes 73728 | tf_op jit(solution)/shard_map/all_gather | solution.py:159
  205.7 0.9 while.153
  207.6 5.7 %all_gather.43 = f32[4,16,128]{2,1,0:T(8,128)S(1)} all-gather(f32[1,16,128]{2,1,0:T(8,128)S(1)} %multiply_multiply_fusion.3), channel_id=1, replica_groups=mesh['gx'=8,'gy'=4] {'gy'}, dimensions={0}, use_global_device_ids=true | all-gather | bytes 40960 | tf_op jit(solution)/shard_map/all_gather | solution.py:172
  213.3 5.4 %all_gather.42 = f32[4,16,128]{2,1,0:T(8,128)S(1)} all-gather(f32[1,16,128]{2,1,0:T(8,128)S(1)} %get-tuple-element.1581), channel_id=1, replica_groups=mesh['gx'=8,'gy'=4] {'gy'}, dimensions={0}, use_global_device_ids=true | all-gather | bytes 40960 | tf_op jit(solution)/shard_map/all_gather | solution.py:171
  218.8 5.2 %all_gather.44 = f32[4,16,128]{2,1,0:T(8,128)S(1)} all-gather(f32[1,16,128]{2,1,0:T(8,128)S(1)} %get-tuple-element.1580), channel_id=1, replica_groups=mesh['gx'=8,'gy'=4] {'gy'}, dimensions={0}, use_global_device_ids=true | all-gather | bytes 40960 | tf_op jit(solution)/shard_map/all_gather | solution.py:168
  223.9 5.2 %all_gather.45 = f32[4,16,128]{2,1,0:T(8,128)S(1)} all-gather(f32[1,16,128]{2,1,0:T(8,128)S(1)} %get-tuple-element.1598), channel_id=1, replica_groups=mesh['gx'=8,'gy'=4] {'gy'}, dimensions={0}, use_global_device_ids=true | all-gather | bytes 40960 | tf_op jit(solution)/shard_map/all_gather | solution.py:169
  229.1 5.2 %all_gather.46 = f32[4,16,128]{2,1,0:T(8,128)S(1)} all-gather(f32[1,16,128]{2,1,0:T(8,128)S(1)} %get-tuple-element.1597), channel_id=1, replica_groups=mesh['gx'=8,'gy'=4] {'gy'}, dimensions={0}, use_global_device_ids=true | all-gather | bytes 40960 | tf_op jit(solution)/shard_map/all_gather | solution.py:173
  234.3 5.2 %all_gather.47 = f32[4,16,128]{2,1,0:T(8,128)S(1)} all-gather(f32[1,16,128]{2,1,0:T(8,128)S(1)} %get-tuple-element.1548), channel_id=1, replica_groups=mesh['gx'=8,'gy'=4] {'gy'}, dimensions={0}, use_global_device_ids=true | all-gather | bytes 40960 | tf_op jit(solution)/shard_map/all_gather | solution.py:170
  240.1 18.7 %while.156 = (s32[]{:T(128)}, f32[256]{0:T(256)S(1)}, f32[1,256]{1,0:T(1,128)S(1)}, f32[128,256]{1,0:T(8,128)S(1)}, f32[128,1,256]{2,1,0:T(1,128)S(1)}, /*index=...) while((s32[]{:T(128)}, f32[256]{0:T(256)S(1)}, ...), condition=%wide.region_13.14_spmd.clone, body=%wide.region_12.13_spmd.clone.sunk | while | flops 2307 | bytes 20616 | solution.py:37
  258.8 4.8 %while.157 = (s32[]{:T(128)}, f32[1,256]{1,0:T(1,128)S(1)}, f32[128,1,256]{2,1,0:T(1,128)S(1)}, f32[128,1,256]{2,1,0:T(1,128)S(1)}, f32[128,256]{1,0:T(8,128)S(1)}, /*index=5*/s32[]{:T(128)}, s32[]{:T(128)}, s32[]{:T(128)}) while((s32[]{:T(128)}, f32[1,256]{1,0:T(1,128)S(1)}, f32[128,1,256]{2,1,0:T(1,128)S(1)}, ...), condition=%wide.region_15.16_spmd.clone, body=%wide.region_14.15_spmd.clone.sunk | while | flops 772 | bytes 5231 | solution.py:44
  (982 shorter events, 22.8 us)
Async XLA Ops:
  1.1 6.4 %copy-start = (f32[16,16,128]{2,1,0:T(8,128)S(1)}, f32[16,16,128]{2,1,0:T(8,128)}, u32[]{:S(2)}) copy-start(f32[16,16,128]{2,1,0:T(8,128)} %param.27) | copy-start | bytes 393220
  1.1 6.4 %copy-start.1 = (f32[16,16,128]{2,1,0:T(8,128)S(1)}, f32[16,16,128]{2,1,0:T(8,128)}, u32[]{:S(2)}) copy-start(f32[16,16,128]{2,1,0:T(8,128)} %param.28) | copy-start | bytes 393220
  1.1 6.7 %collective-permute-start = (f32[2,1,16,128]{3,1,2,0:T(1,128)S(1)}, f32[2,1,16,128]{3,1,2,0:T(1,128)S(1)}, u32[]{:S(2)}, u32[]{:S(2)}) collective-permute-start(f32[2,1,16,128]{3,1,2,0:T(1,128)S(1)} %get-tuple-element.1588), channel_id=1, source_target_pairs={{0,4},{4,8},{8,12},{12,16},{16,20},{20,24},{24,28},{1,5},{5,9},{9,... | collective-permute-start | bytes 49160 | tf_op jit(solution)/shard_map/ppermute | solution.py:15
  6.1 5.6 %collective-permute-start.1 = (f32[2,1,16,128]{3,1,2,0:T(1,128)S(1)}, f32[2,1,16,128]{3,1,2,0:T(1,128)S(1)}, u32[]{:S(2)}, u32[]{:S(2)}) collective-permute-start(f32[2,1,16,128]{3,1,2,0:T(1,128)S(1)} %get-tuple-element.1589), channel_id=1, source_target_pairs={{4,0},{8,4},{12,8},{16,12},{20,16},{24,20},{28,24},{5,1},{9,5},{13... | collective-permute-start | bytes 49160 | tf_op jit(solution)/shard_map/ppermute | solution.py:17
  11.8 3.2 %collective-permute-start.2 = (f32[2,18,1,128]{3,1,2,0:T(8,128)S(1)}, f32[2,18,1,128]{3,1,2,0:T(8,128)S(1)}, u32[]{:S(2)}, u32[]{:S(2)}) collective-permute-start(f32[2,18,1,128]{3,1,2,0:T(8,128)S(1)} %get-tuple-element.1586), channel_id=1, source_target_pairs={{0,1},{1,2},{2,3},{4,5},{5,6},{6,7},{8,9},{9,10},{10,11},{12,13},{... | collective-permute-start | bytes 55304 | tf_op jit(solution)/shard_map/ppermute | solution.py:15
  13.1 4.8 %collective-permute-start.3 = (f32[2,18,1,128]{3,1,2,0:T(8,128)S(1)}, f32[2,18,1,128]{3,1,2,0:T(8,128)S(1)}, u32[]{:S(2)}, u32[]{:S(2)}) collective-permute-start(f32[2,18,1,128]{3,1,2,0:T(8,128)S(1)} %get-tuple-element.1587), channel_id=1, source_target_pairs={{1,0},{2,1},{3,2},{5,4},{6,5},{7,6},{9,8},{10,9},{11,10},{13,12},{... | collective-permute-start | bytes 55304 | tf_op jit(solution)/shard_map/ppermute | solution.py:17
  18.3 0.9 copy-start.2
where the time goes:
time: 265 us; the launch traced here: 264 us
  blocking collectives  215 us (81%)
  local copies, waits for them, and re-layouts  12.3 us (5%)
  loops' own time  10.3 us (4%)
  other arithmetic  10.1 us (4%)
  starting transfers between devices  8.88 us (3%)
  waiting for transfers between devices  6.84 us (3%)
    all_gather x1, blocking collectives, couple_x(): lax.all_gather(coeffs[4][None], 'gx', axis=0, tiled=True)  30.9 us
    all_gather x1, blocking collectives, couple_x(): lax.all_gather(coeffs[3][None], 'gx', axis=0, tiled=True)  30.5 us
    all_gather x1, blocking collectives, couple_x(): lax.all_gather(coeffs[0][None], 'gx', axis=0, tiled=True)  30.5 us
    all_gather x1, blocking collectives, couple_x(): lax.all_gather(coeffs[1][None], 'gx', axis=0, tiled=True)  30.5 us
    all_gather x1, blocking collectives, couple_x(): lax.all_gather(coeffs[5][None], 'gx', axis=0, tiled=True)  30.5 us
    all_gather x1, blocking collectives, couple_x(): lax.all_gather(coeffs[2][None], 'gx', axis=0, tiled=True)  30.5 us
    ppermute x2, waiting for transfers between devices, padded_2(): lax.ppermute(head, axis, [((i + 1) % count, i) for i in range(ends)])  6.84 us
    another operation x3, loops' own time, thomas(): lax.scan(forward_step, start, (lower, diag, upper, stacked))  6.57 us
  transfers between devices with their start and end apart: 4, of which 2 were waited for; matrix products, arithmetic and copies ran while one was open for 0% of the time, Pallas kernels for 0%

commit v1 on v0

v1 whole, which is shorter than its diff:
```python
import functools

import jax
import jax.numpy as jnp
from jax import lax
from jax.experimental import pallas as pl
from jax.experimental.pallas import tpu as pltpu
from jax.sharding import PartitionSpec as P

MESH = pl.DeviceIdType.MESH


def factor(cells, first, last):
    count = len(cells)
    ones = jnp.ones_like(cells[0])
    excess = jnp.where(first, 1.0 + 0.25 * cells[0], ones)
    mults, inverses = [None], []
    for i in range(count):
        if i == count - 1:
            excess = excess + jnp.where(last, 0.25 * cells[i], 0.0)
            inverses.append(1.0 / excess)
        else:
            face = 0.25 * (cells[i] + cells[i + 1])
            inverse = 1.0 / (excess + face)
            mult = face * inverse
            inverses.append(inverse)
            mults.append(mult)
            excess = 1.0 + mult * excess
    from_last = [None] * count
    from_last[-1] = inverses[-1]
    for i in range(count - 2, -1, -1):
        from_last[i] = mults[i + 1] * from_last[i + 1]
    prods = [ones]
    for i in range(1, count):
        prods.append(mults[i] * prods[-1])
    from_first = [None] * count
    from_first[-1] = prods[-1] * inverses[-1]
    for i in range(count - 2, -1, -1):
        from_first[i] = prods[i] * inverses[i] + mults[i + 1] * from_first[i + 1]
    return mults, inverses, from_first, from_last


def substitute(rights, mults, inverses):
    count = len(rights)
    values = [rights[0]]
    for i in range(1, count):
        values.append(rights[i] + mults[i] * values[-1])
    out = [None] * count
    out[-1] = values[-1] * inverses[-1]
    for i in range(count - 2, -1, -1):
        out[i] = values[i] * inverses[i] + mults[i + 1] * out[i + 1]
    return out


def kernel(nx, ny, lx, ly, depth, f_ref, c_ref, s_ref, o_ref,
           mult_x, inv_x, head_x, tail_x, mult_y, inv_y, head_y, tail_y,
           pcr_lo, pcr_hi, pcr_inv, work, halo_out, halo_in,
           mat_x, mat_y, alpha_x, beta_x, alpha_y, beta_y, own_x, own_y,
           part_x, part_y, out_x, out_y,
           hs_sem, hr_sem, mxs_sem, mxr_sem, mys_sem, myr_sem,
           pxs_sem, pxr_sem, pys_sem, pyr_sem):
    ix = lax.axis_index("gx")
    iy = lax.axis_index("gy")

    def peer_x(k):
        return (lax.rem(ix + k, nx), iy)

    def peer_y(k):
        return (ix, lax.rem(iy + k, ny))

    barrier = pltpu.get_barrier_semaphore()
    for k in range(1, nx):
        pl.semaphore_signal(barrier, inc=1, device_id=peer_x(k), device_id_type=MESH)
    for k in range(1, ny):
        pl.semaphore_signal(barrier, inc=1, device_id=peer_y(k), device_id_type=MESH)

    def row_x(i):
        return pl.ds(i * ly, ly)

    def row_y(j):
        return pl.ds(j, lx, stride=ly)

    def keep(refs, lists):
        for ref, items in zip(refs, lists):
            for i, item in enumerate(items):
                if item is not None:
                    ref[i] = item

    def describe(mat, index, cells, heads, tails):
        mat[index, 0] = heads[0]
        mat[index, 1] = tails[0]
        mat[index, 2] = tails[-1]
        mat[index, 3] = cells[0]
        mat[index, 4] = cells[-1]

    def spread(src_of, table, index, peer, count, s_sem, r_sem):
        copies = []
        for k in range(1, count):
            copy = pltpu.make_async_remote_copy(
                src_ref=src_of(k), dst_ref=table.at[index],
                send_sem=s_sem.at[k - 1], recv_sem=r_sem.at[k - 1],
                device_id=peer(k), device_id_type=MESH)
            copy.start()
            copies.append(copy)
        return copies

    cells = [c_ref[row_x(i)] for i in range(lx)]
    parts = factor(cells, ix == 0, ix == nx - 1)
    keep((mult_x, inv_x, head_x, tail_x), parts)
    describe(mat_x, ix, cells, parts[2], parts[3])
    for side, j in ((0, 0), (1, ly - 1)):
        halo_out[side, 0] = f_ref[row_y(j)]
        halo_out[side, 1] = c_ref[row_y(j)]

    pl.semaphore_wait(barrier, nx + ny - 2)

    halos = []
    for side, k in ((0, ny - 1), (1, 1)):
        copy = pltpu.make_async_remote_copy(
            src_ref=halo_out.at[side], dst_ref=halo_in.at[side],
            send_sem=hs_sem.at[side], recv_sem=hr_sem.at[side],
            device_id=peer_y(k), device_id_type=MESH)
        copy.start()
        halos.append(copy)
    mats_x = spread(lambda k: mat_x.at[ix], mat_x, ix, peer_x, nx, mxs_sem, mxr_sem)

    cells_y = [c_ref[row_y(j)] for j in range(ly)]
    parts = factor(cells_y, iy == 0, iy == ny - 1)
    keep((mult_y, inv_y, head_y, tail_y), parts)
    describe(mat_y, iy, cells_y, parts[2], parts[3])
    mats_y = spread(lambda k: mat_y.at[iy], mat_y, iy, peer_y, ny, mys_sem, myr_sem)

    lane = lax.broadcasted_iota(jnp.int32, (ly, depth), 1)
    low_end = lane == 0
    high_end = lane == depth - 1
    for i in range(lx):
        cond = c_ref[row_x(i)]
        value = f_ref[row_x(i)]
        lo = jnp.where(low_end, 0.0, 0.25 * (cond + pltpu.roll(cond, 1, 1)))
        hi = jnp.where(high_end, 0.0, 0.25 * (cond + pltpu.roll(cond, depth - 1, 1)))
        edge = jnp.where(low_end, 0.25 * cond, 0.0) + jnp.where(high_end, 0.25 * cond, 0.0)
        flux = (hi * (pltpu.roll(value, depth - 1, 1) - value)
                - lo * (value - pltpu.roll(value, 1, 1)) - edge * value)
        work[row_x(i)] = 2.0 * (value + flux) + s_ref[row_x(i)]
        excess = 1.0 + edge
        shift, level = 1, 0
        while shift < depth:
            inverse = 1.0 / (excess + lo + hi)
            a = lo * pltpu.roll(inverse, shift, 1)
            b = hi * pltpu.roll(inverse, depth - shift, 1)
            pcr_lo[level, row_x(i)] = a
            pcr_hi[level, row_x(i)] = b
            excess = (excess + a * pltpu.roll(excess, shift, 1)
                      + b * pltpu.roll(excess, depth - shift, 1))
            lo = a * pltpu.roll(lo, shift, 1)
            hi = b * pltpu.roll(hi, depth - shift, 1)
            shift, level = 2 * shift, level + 1
        pcr_inv[row_x(i)] = 1.0 / (excess + lo + hi)

    for copy in halos:
        copy.wait()
    below_f = jnp.where(iy == 0, 0.0, halo_in[1, 0])
    below_c = jnp.where(iy == 0, 0.0, halo_in[1, 1])
    above_f = jnp.where(iy == ny - 1, 0.0, halo_in[0, 0])
    above_c = jnp.where(iy == ny - 1, 0.0, halo_in[0, 1])
    value = f_ref[row_y(0)]
    cond = c_ref[row_y(0)]
    flux_lo = 0.5 * (below_c + cond) * (value - below_f)
    for j in range(ly):
        if j == ly - 1:
            next_f, next_c = above_f, above_c
        else:
            next_f, next_c = f_ref[row_y(j + 1)], c_ref[row_y(j + 1)]
        flux_hi = 0.5 * (cond + next_c) * (next_f - value)
        work[row_y(j)] += flux_hi - flux_lo
        value, cond, flux_lo = next_f, next_c, flux_hi

    def chains(mat, count, alpha, beta, own, index):
        links = [4.0 / (mat[k, 4] + mat[k + 1, 3]) for k in range(count - 1)]
        zeros = jnp.zeros_like(links[0])
        alpha[0] = zeros
        own[0, 0] = zeros
        joined = mat[0, 2]
        for k in range(1, count):
            inverse = 1.0 / (links[k - 1] + joined + mat[k, 0])
            ratio = mat[k, 1] * inverse
            alpha[k] = ratio
            own[0, k] = inverse
            joined = mat[k, 2] - mat[k, 1] * ratio
        beta[count - 1] = zeros
        own[1, count - 1] = zeros
        joined = mat[count - 1, 0]
        for k in range(count - 2, -1, -1):
            inverse = 1.0 / (links[k] + joined + mat[k, 2])
            ratio = mat[k, 1] * inverse
            beta[k] = ratio
            own[1, k] = inverse
            joined = mat[k, 0] - mat[k, 1] * ratio

    def send_parts(head, tail, alpha, beta, index, count, outs, table, peer, s_sem, r_sem):
        outs[0] = tail - alpha[index] * head
        outs[1] = head - beta[index] * tail
        table[index] = head

        def src_of(k):
            return outs.at[lax.div(index + k, count)]
        return spread(src_of, table, index, peer, count, s_sem, r_sem)

    def fluxes(head, tail, alpha, beta, own, index, count, table):
        before = jnp.zeros_like(head)
        for k in range(count - 1):
            before = jnp.where(k < index, alpha[k] * before + table[k], before)
        after = jnp.zeros_like(head)
        for k in range(count - 1, 0, -1):
            after = jnp.where(k > index, beta[k] * after + table[k], after)
        a, b = alpha[index], beta[index]
        scale = 1.0 / (1.0 - a * b)
        left = before - head
        right = tail - after
        into = scale * own[0, index] * (left + b * right)
        out = scale * own[1, index] * (right + a * left)
        return into, out

    local = substitute([work[row_x(i)] for i in range(lx)],
                       [None] + [mult_x[i] for i in range(1, lx)],
                       [inv_x[i] for i in range(lx)])
    for copy in mats_x:
        copy.wait()
    chains(mat_x, nx, alpha_x, beta_x, own_x, ix)
    copies = send_parts(local[0], local[-1], alpha_x, beta_x, ix, nx,
                        out_x, part_x, peer_x, pxs_sem, pxr_sem)
    for i in range(lx):
        work[row_x(i)] = local[i] - 2.0 * f_ref[row_x(i)]
    head, tail = local[0], local[-1]
    for copy in mats_y:
        copy.wait()
    chains(mat_y, ny, alpha_y, beta_y, own_y, iy)
    for copy in copies:
        copy.wait()
    into, out = fluxes(head, tail, alpha_x, beta_x, own_x, ix, nx, part_x)
    for i in range(lx):
        work[row_x(i)] += into * head_x[i] - out * tail_x[i]

    local = substitute([work[row_y(j)] for j in range(ly)],
                       [None] + [mult_y[j] for j in range(1, ly)],
                       [inv_y[j] for j in range(ly)])
    copies = send_parts(local[0], local[-1], alpha_y, beta_y, iy, ny,
                        out_y, part_y, peer_y, pys_sem, pyr_sem)
    for j in range(ly):
        work[row_y(j)] = local[j]
    head, tail = local[0], local[-1]
    for copy in copies:
        copy.wait()
    into, out = fluxes(head, tail, alpha_y, beta_y, own_y, iy, ny, part_y)
    for j in range(ly):
        work[row_y(j)] += into * head_y[j] - out * tail_y[j]

    shift, level = 1, 0
    right = work[...]
    while shift < depth:
        right = (right + pcr_lo[level] * pltpu.roll(right, shift, 1)
                 + pcr_hi[level] * pltpu.roll(right, depth - shift, 1))
        shift, level = 2 * shift, level + 1
    o_ref[...] = f_ref[...] + right * pcr_inv[...]


def solution(mesh):
    nx, ny = mesh.shape["gx"], mesh.shape["gy"]

    def body(field, conductance, source):
        lx, ly, depth = field.shape
        lines = lx * ly
        levels = max(1, (depth - 1).bit_length())
        f32 = jnp.float32

        def vmem(*shape):
            return pltpu.VMEM(shape, f32)

        def dma(count):
            return pltpu.SemaphoreType.DMA((count,))

        along_x = [vmem(lx, ly, depth)] * 4
        along_y = [vmem(ly, lx, depth)] * 4
        out = pl.pallas_call(
            functools.partial(kernel, nx, ny, lx, ly, depth),
            out_shape=jax.ShapeDtypeStruct((lines, depth), f32),
            in_specs=[pl.BlockSpec(memory_space=pltpu.VMEM)] * 3,
            out_specs=pl.BlockSpec(memory_space=pltpu.VMEM),
            scratch_shapes=along_x + along_y + [
                vmem(levels, lines, depth), vmem(levels, lines, depth), vmem(lines, depth),
                vmem(lines, depth), vmem(2, 2, lx, depth), vmem(2, 2, lx, depth),
                vmem(nx, 5, ly, depth), vmem(ny, 5, lx, depth),
                vmem(nx, ly, depth), vmem(nx, ly, depth),
                vmem(ny, lx, depth), vmem(ny, lx, depth),
                vmem(2, nx, ly, depth), vmem(2, ny, lx, depth),
                vmem(nx, ly, depth), vmem(ny, lx, depth),
                vmem(2, ly, depth), vmem(2, lx, depth),
                dma(2), dma(2), dma(nx - 1), dma(nx - 1), dma(ny - 1), dma(ny - 1),
                dma(nx - 1), dma(nx - 1), dma(ny - 1), dma(ny - 1),
            ],
            compiler_params=pltpu.CompilerParams(collective_id=0, has_side_effects=True),
            name="step",
        )(field.reshape(lines, depth), conductance.reshape(lines, depth),
          source.reshape(lines, depth))
        return out.reshape(lx, ly, depth)

    spec = P("gx", "gy", None)
    return jax.shard_map(body, mesh=mesh, in_specs=(spec, spec, spec), out_specs=spec,
                         check_vma=False)
```

time: 265 us -> 27.2 us (0.10)
  blocking collectives: 215 us -> 0 us
  Pallas kernels: 0 us -> 25.5 us
  local copies, waits for them, and re-layouts: 12.3 us -> 1.57 us
  loops' own time: 10.3 us -> 0 us
  other arithmetic: 10.1 us -> 0 us
  starting transfers between devices: 8.88 us -> 0 us
  waiting for transfers between devices: 6.84 us -> 0 us
    all_gather x12 -> x0, blocking collectives: 215 us -> none  [the longest x1 30.9 us: couple_x(): lax.all_gather(coeffs[4][None], 'gx', axis=0, tiled=True)]
    pallas_call x0 -> x1, Pallas kernels: none -> 25.5 us  [body(): pl.pallas_call(functools.partial(kernel, nx, ny, lx, ly, depth), out_shap...]
    another operation x8 -> x0, loops' own time: 10.3 us -> none  [the longest x3 6.57 us: thomas(): lax.scan(forward_step, start, (lower, diag, upper, stacked))]
    ppermute x4 -> x0, starting transfers between devices: 8.88 us -> none  [the longest x2 6.29 us: padded_2(): lax.ppermute(tail, axis, [(i, (i + 1) % count) for i in range(ends)])]
    ppermute x4 -> x0, waiting for transfers between devices: 6.84 us -> none  [the longest x2 6.84 us: padded_2(): lax.ppermute(head, axis, [((i + 1) % count, i) for i in range(ends)])]
    dynamic_update_slice x340 -> x0, other arithmetic: 6.32 us -> none  [thomas(): lax.scan(forward_step, start, (lower, diag, upper, stacked))]
    dynamic_update_slice x128 -> x0, local copies, waits for them, and re-layouts: 5.52 us -> none  [thomas(): lax.scan(forward_step, start, (lower, diag, upper, stacked))]
    dynamic_slice x256 -> x0, local copies, waits for them, and re-layouts: 2.9 us -> none  [thomas(): lax.scan(forward_step, start, (lower, diag, upper, stacked))]
  transfers between devices with their start and end apart: 4 -> 0, of which waited for: 2 -> 0; matrix products, arithmetic and copies ran while one was open for 0% -> 0% of each run, Pallas kernels for 0% -> 0%
where the time goes in v1:
time: 27.2 us; the launch traced here: 27.1 us
  Pallas kernels  25.5 us (94%)
  local copies, waits for them, and re-layouts  1.57 us (6%)
    pallas_call x1, Pallas kernels, body(): pl.pallas_call(functools.partial(kernel, nx, ny, lx, ly, depth), out_shap...  25.5 us
    unnamed x1, local copies, waits for them, and re-layouts  1.57 us

profile of v1, /device:TPU:0, one launch (start us, length us, event | category | flops | bytes accessed | tf_op | source)
XLA Modules:
  0.0 27.1 jit_solution(16740380087073210934)
XLA Ops:
  0.0 25.5 %step.1 = f32[256,128]{1,0:T(8,128)} custom-call(f32[256,128]{1,0:T(8,128)} %bitcast.5, f32[256,128]{1,0:T(8,128)} %bitcast.6, f32[256,128]{1,0:T(8,128)} %bitcast.7), custom_call_target="tpu_custom_call" | custom-call | tf_op jit(solution)/shard_map/step/pallas_call | solution.py:284
  25.5 1.6 %copy.5 = f32[16,16,128]{2,1,0:T(8,128)} copy(f32[16,16,128]{2,1,0:T(8,128)} %bitcast.4) | data formatting | bytes 262144

commit v2 on v1

v2 whole, which is shorter than its diff:
```python
import functools

import jax
import jax.numpy as jnp
from jax import lax
from jax.experimental import pallas as pl
from jax.experimental.pallas import tpu as pltpu
from jax.sharding import PartitionSpec as P

MESH = pl.DeviceIdType.MESH


def factor(cells, first, last):
    count = len(cells)
    ones = jnp.ones_like(cells[0])
    excess = jnp.where(first, 1.0 + 0.25 * cells[0], ones)
    mults, inverses = [None], []
    for i in range(count):
        if i == count - 1:
            excess = excess + jnp.where(last, 0.25 * cells[i], 0.0)
            inverses.append(1.0 / excess)
        else:
            face = 0.25 * (cells[i] + cells[i + 1])
            inverse = 1.0 / (excess + face)
            mult = face * inverse
            inverses.append(inverse)
            mults.append(mult)
            excess = 1.0 + mult * excess
    from_last = [None] * count
    from_last[-1] = inverses[-1]
    for i in range(count - 2, -1, -1):
        from_last[i] = mults[i + 1] * from_last[i + 1]
    prods = [ones]
    for i in range(1, count):
        prods.append(mults[i] * prods[-1])
    from_first = [None] * count
    from_first[-1] = prods[-1] * inverses[-1]
    for i in range(count - 2, -1, -1):
        from_first[i] = prods[i] * inverses[i] + mults[i + 1] * from_first[i + 1]
    return mults, inverses, from_first, from_last


def substitute(rights, mults, inverses):
    count = len(rights)
    values = [rights[0]]
    for i in range(1, count):
        values.append(rights[i] + mults[i] * values[-1])
    out = [None] * count
    out[-1] = values[-1] * inverses[-1]
    for i in range(count - 2, -1, -1):
        out[i] = values[i] * inverses[i] + mults[i + 1] * out[i + 1]
    return out


def kernel(nx, ny, lx, ly, depth, f_hbm, c_hbm, s_hbm, o_ref,
           f_ref, c_ref, s_ref,
           mult_x, inv_x, head_x, tail_x, mult_y, inv_y, head_y, tail_y,
           pcr_lo, pcr_hi, pcr_inv, work, halo_out, halo_in,
           mat_x, mat_y, outer_x, inner_x, alpha_y, beta_y, own_y,
           part_x, part_y, out_y, mid_out, mid_in, chain_out, chain_in,
           in_sem, hs_sem, hr_sem, mxs_sem, mxr_sem, mys_sem, myr_sem,
           pxs_sem, pxr_sem, pys_sem, pyr_sem, mid_sem):
    ix = lax.axis_index("gx")
    iy = lax.axis_index("gy")
    half = nx // 2
    upper = lax.div(ix, half)
    place = ix - upper * half
    rank = ix + upper * (nx - 1 - 2 * ix)
    flip = upper == 1

    def peer_x(k):
        return (upper * half + lax.rem(place + k, half), iy)

    mirror = (lax.rem(ix + half, nx), iy)

    def peer_y(k):
        return (ix, lax.rem(iy + k, ny))

    barrier = pltpu.get_barrier_semaphore()
    pl.semaphore_signal(barrier, inc=1, device_id=mirror, device_id_type=MESH)
    for k in range(1, half):
        pl.semaphore_signal(barrier, inc=1, device_id=peer_x(k), device_id_type=MESH)
    for k in range(1, ny):
        pl.semaphore_signal(barrier, inc=1, device_id=peer_y(k), device_id_type=MESH)

    fetches = []
    for n, (src, dst) in enumerate(((c_hbm, c_ref), (f_hbm, f_ref), (s_hbm, s_ref))):
        fetch = pltpu.make_async_copy(src, dst, in_sem.at[n])
        fetch.start()
        fetches.append(fetch)

    def row_x(i):
        return pl.ds(i * ly, ly)

    def row_y(j):
        return pl.ds(j, lx, stride=ly)

    def keep(refs, lists):
        for ref, items in zip(refs, lists):
            for i, item in enumerate(items):
                if item is not None:
                    ref[i] = item

    def remote(src, dst, s_sem, r_sem, device):
        copy = pltpu.make_async_remote_copy(
            src_ref=src, dst_ref=dst, send_sem=s_sem, recv_sem=r_sem,
            device_id=device, device_id_type=MESH)
        copy.start()
        return copy

    def spread(src_of, table, index, peer, count, s_sem, r_sem):
        return [remote(src_of(k), table.at[index], s_sem.at[k - 1], r_sem.at[k - 1], peer(k))
                for k in range(1, count)]

    def turn(first, second):
        return jnp.where(flip, second, first), jnp.where(flip, first, second)

    fetches[0].wait()
    cells = [c_ref[row_x(i)] for i in range(lx)]
    parts = factor(cells, ix == 0, ix == nx - 1)
    keep((mult_x, inv_x, head_x, tail_x), parts)
    heads, tails = parts[2], parts[3]
    mat_x[rank, 0], mat_x[rank, 2] = turn(heads[0], tails[-1])
    mat_x[rank, 1] = tails[0]
    mat_x[rank, 3], mat_x[rank, 4] = turn(cells[0], cells[-1])
    fetches[1].wait()
    for side, j in ((0, 0), (1, ly - 1)):
        halo_out[side, 0] = f_ref[row_y(j)]
        halo_out[side, 1] = c_ref[row_y(j)]

    pl.semaphore_wait(barrier, half + ny - 1)

    halos = [remote(halo_out.at[side], halo_in.at[side], hs_sem.at[side], hr_sem.at[side],
                    peer_y(k)) for side, k in ((0, ny - 1), (1, 1))]
    mats_x = spread(lambda k: mat_x.at[rank], mat_x, rank, peer_x, half, mxs_sem, mxr_sem)

    cells = [c_ref[row_y(j)] for j in range(ly)]
    parts = factor(cells, iy == 0, iy == ny - 1)
    keep((mult_y, inv_y, head_y, tail_y), parts)
    heads, tails = parts[2], parts[3]
    mat_y[iy, 0] = heads[0]
    mat_y[iy, 1] = tails[0]
    mat_y[iy, 2] = tails[-1]
    mat_y[iy, 3] = cells[0]
    mat_y[iy, 4] = cells[-1]
    mats_y = spread(lambda k: mat_y.at[iy], mat_y, iy, peer_y, ny, mys_sem, myr_sem)

    lane = lax.broadcasted_iota(jnp.int32, (ly, depth), 1)
    low_end = lane == 0
    high_end = lane == depth - 1

    def faces_z(cond):
        lo = jnp.where(low_end, 0.0, 0.25 * (cond + pltpu.roll(cond, 1, 1)))
        hi = jnp.where(high_end, 0.0, 0.25 * (cond + pltpu.roll(cond, depth - 1, 1)))
        edge = jnp.where(low_end, 0.25 * cond, 0.0) + jnp.where(high_end, 0.25 * cond, 0.0)
        return lo, hi, edge

    fetches[2].wait()
    for i in range(lx):
        value = f_ref[row_x(i)]
        lo, hi, edge = faces_z(c_ref[row_x(i)])
        flux = (hi * (pltpu.roll(value, depth - 1, 1) - value)
                - lo * (value - pltpu.roll(value, 1, 1)) - edge * value)
        work[row_x(i)] = 2.0 * (value + flux) + s_ref[row_x(i)]

    for copy in halos:
        copy.wait()
    below_f = jnp.where(iy == 0, 0.0, halo_in[1, 0])
    below_c = jnp.where(iy == 0, 0.0, halo_in[1, 1])
    above_f = jnp.where(iy == ny - 1, 0.0, halo_in[0, 0])
    above_c = jnp.where(iy == ny - 1, 0.0, halo_in[0, 1])
    value = f_ref[row_y(0)]
    cond = c_ref[row_y(0)]
    flux_lo = 0.5 * (below_c + cond) * (value - below_f)
    for j in range(ly):
        if j == ly - 1:
            next_f, next_c = above_f, above_c
        else:
            next_f, next_c = f_ref[row_y(j + 1)], c_ref[row_y(j + 1)]
        flux_hi = 0.5 * (cond + next_c) * (next_f - value)
        work[row_y(j)] += flux_hi - flux_lo
        value, cond, flux_lo = next_f, next_c, flux_hi

    local = substitute([work[row_x(i)] for i in range(lx)],
                       [None] + [mult_x[i] for i in range(1, lx)],
                       [inv_x[i] for i in range(lx)])
    near, far = turn(local[0], local[-1])
    part_x[rank, 0] = near
    part_x[rank, 1] = far
    parts_x = spread(lambda k: part_x.at[rank], part_x, rank, peer_x, half, pxs_sem, pxr_sem)
    for i in range(lx):
        work[row_x(i)] = local[i] - 2.0 * f_ref[row_x(i)]

    for i in range(lx):
        lo, hi, edge = faces_z(c_ref[row_x(i)])
        excess = 1.0 + edge
        shift, level = 1, 0
        while shift < depth:
            inverse = 1.0 / (excess + lo + hi)
            a = lo * pltpu.roll(inverse, shift, 1)
            b = hi * pltpu.roll(inverse, depth - shift, 1)
            pcr_lo[level, row_x(i)] = a
            pcr_hi[level, row_x(i)] = b
            excess = (excess + a * pltpu.roll(excess, shift, 1)
                      + b * pltpu.roll(excess, depth - shift, 1))
            lo = a * pltpu.roll(lo, shift, 1)
            hi = b * pltpu.roll(hi, depth - shift, 1)
            shift, level = 2 * shift, level + 1
        pcr_inv[row_x(i)] = 1.0 / (excess + lo + hi)

    for copy in mats_x:
        copy.wait()
    zeros = jnp.zeros_like(near)
    outer_x[0, 0] = zeros
    outer_x[1, 0] = zeros
    outer_x[2, 0] = zeros
    ratios = [zeros]
    joined = mat_x[0, 2]
    for q in range(1, half):
        link = 4.0 / (mat_x[q - 1, 4] + mat_x[q, 3])
        inverse = 1.0 / (link + joined + mat_x[q, 0])
        ratio = mat_x[q, 1] * inverse
        outer_x[0, q] = inverse
        outer_x[1, q] = ratio
        ratios.append(ratio)
        joined = mat_x[q, 2] - mat_x[q, 1] * ratio
    mid_out[0] = joined
    mid_out[1] = mat_x[half - 1, 4]
    mids = remote(mid_out, mid_in, mid_sem.at[0], mid_sem.at[1], mirror)

    for copy in mats_y:
        copy.wait()
    links = [4.0 / (mat_y[k, 4] + mat_y[k + 1, 3]) for k in range(ny - 1)]
    blank = jnp.zeros_like(links[0])
    alpha_y[0] = blank
    own_y[0, 0] = blank
    joined = mat_y[0, 2]
    for k in range(1, ny):
        inverse = 1.0 / (links[k - 1] + joined + mat_y[k, 0])
        ratio = mat_y[k, 1] * inverse
        alpha_y[k] = ratio
        own_y[0, k] = inverse
        joined = mat_y[k, 2] - mat_y[k, 1] * ratio
    beta_y[ny - 1] = blank
    own_y[1, ny - 1] = blank
    joined = mat_y[ny - 1, 0]
    for k in range(ny - 2, -1, -1):
        inverse = 1.0 / (links[k] + joined + mat_y[k, 2])
        ratio = mat_y[k, 1] * inverse
        beta_y[k] = ratio
        own_y[1, k] = inverse
        joined = mat_y[k, 0] - mat_y[k, 1] * ratio

    for copy in parts_x:
        copy.wait()
    before = part_x[0, 1]
    for q in range(1, half):
        outer_x[2, q] = before
        before = part_x[q, 1] + ratios[q] * (before - part_x[q, 0])
    chain_out[...] = before
    chained = remote(chain_out, chain_in, mid_sem.at[2], mid_sem.at[3], mirror)

    mids.wait()
    joined = mid_in[0]
    beyond = mid_in[1]
    ratios = [None] * half
    for q in range(half - 1, -1, -1):
        inverse = 1.0 / (4.0 / (mat_x[q, 4] + beyond) + joined + mat_x[q, 2])
        ratio = mat_x[q, 1] * inverse
        inner_x[0, q] = inverse
        inner_x[1, q] = ratio
        ratios[q] = ratio
        joined = mat_x[q, 0] - mat_x[q, 1] * ratio
        beyond = mat_x[q, 3]
    a, b = outer_x[1, rank], inner_x[1, rank]
    scale = 1.0 / (1.0 - a * b)
    gain_near = scale * outer_x[0, rank]
    gain_far = scale * inner_x[0, rank]
    left = outer_x[2, rank] - near
    chained.wait()
    after = chain_in[...]
    for q in range(half - 1, -1, -1):
        inner_x[2, q] = after
        if q:
            after = part_x[q, 0] + ratios[q] * (after - part_x[q, 1])
    right = far - inner_x[2, rank]
    into = gain_near * (left + b * right)
    out = gain_far * (right + a * left)
    on_head, on_tail = turn(into, -out)
    for i in range(lx):
        work[row_x(i)] += on_head * head_x[i] + on_tail * tail_x[i]

    local = substitute([work[row_y(j)] for j in range(ly)],
                       [None] + [mult_y[j] for j in range(1, ly)],
                       [inv_y[j] for j in range(ly)])
    head, tail = local[0], local[-1]
    a, b = alpha_y[iy], beta_y[iy]
    out_y[0] = tail - a * head
    out_y[1] = head - b * tail
    part_y[iy] = head
    copies = spread(lambda k: out_y.at[lax.div(iy + k, ny)], part_y, iy, peer_y, ny,
                    pys_sem, pyr_sem)
    for j in range(ly):
        work[row_y(j)] = local[j]
    scale = 1.0 / (1.0 - a * b)
    gain_in, gain_out = scale * own_y[0, iy], scale * own_y[1, iy]
    for copy in copies:
        copy.wait()
    before = blank
    for k in range(ny - 1):
        before = jnp.where(k < iy, alpha_y[k] * before + part_y[k], before)
    after = blank
    for k in range(ny - 1, 0, -1):
        after = jnp.where(k > iy, beta_y[k] * after + part_y[k], after)
    left = before - head
    right = tail - after
    into = gain_in * (left + b * right)
    out = gain_out * (right + a * left)
    for j in range(ly):
        work[row_y(j)] += into * head_y[j] - out * tail_y[j]

    shift, level = 1, 0
    right = work[...]
    while shift < depth:
        right = (right + pcr_lo[level] * pltpu.roll(right, shift, 1)
                 + pcr_hi[level] * pltpu.roll(right, depth - shift, 1))
        shift, level = 2 * shift, level + 1
    o_ref[...] = f_ref[...] + right * pcr_inv[...]


def solution(mesh):
    nx, ny = mesh.shape["gx"], mesh.shape["gy"]

    def body(field, conductance, source):
        lx, ly, depth = field.shape
        lines = lx * ly
        levels = max(1, (depth - 1).bit_length())
        f32 = jnp.float32

        def vmem(*shape):
            return pltpu.VMEM(shape, f32)

        def dma(count):
            return pltpu.SemaphoreType.DMA((count,))

        half = nx // 2
        along_x = [vmem(lx, ly, depth)] * 4
        along_y = [vmem(ly, lx, depth)] * 4
        out = pl.pallas_call(
            functools.partial(kernel, nx, ny, lx, ly, depth),
            out_shape=jax.ShapeDtypeStruct((lines, depth), f32),
            in_specs=[pl.BlockSpec(memory_space=pltpu.HBM)] * 3,
            out_specs=pl.BlockSpec(memory_space=pltpu.VMEM),
            scratch_shapes=[vmem(lines, depth)] * 3 + along_x + along_y + [
                vmem(levels, lines, depth), vmem(levels, lines, depth), vmem(lines, depth),
                vmem(lines, depth), vmem(2, 2, lx, depth), vmem(2, 2, lx, depth),
                vmem(half, 5, ly, depth), vmem(ny, 5, lx, depth),
                vmem(3, half, ly, depth), vmem(3, half, ly, depth),
                vmem(ny, lx, depth), vmem(ny, lx, depth), vmem(2, ny, lx, depth),
                vmem(half, 2, ly, depth), vmem(ny, lx, depth), vmem(2, lx, depth),
                vmem(2, ly, depth), vmem(2, ly, depth), vmem(ly, depth), vmem(ly, depth),
                dma(3), dma(2), dma(2), dma(half - 1), dma(half - 1), dma(ny - 1), dma(ny - 1),
                dma(half - 1), dma(half - 1), dma(ny - 1), dma(ny - 1), dma(4),
            ],
            compiler_params=pltpu.CompilerParams(
                collective_id=0, has_side_effects=True),
            name="step",
        )(field.reshape(lines, depth), conductance.reshape(lines, depth),
          source.reshape(lines, depth))
        return out.reshape(lx, ly, depth)

    spec = P("gx", "gy", None)
    return jax.shard_map(body, mesh=mesh, in_specs=(spec, spec, spec), out_specs=spec,
                         check_vma=False)
```

time: 27.2 us -> 22 us (0.81)
  Pallas kernels: 25.5 us -> 20.3 us
    pallas_call x1, Pallas kernels: 25.5 us -> 20.3 us  [body(): pl.pallas_call(functools.partial(kernel, nx, ny, lx, ly, depth), out_shap...]
where the time goes in v2:
time: 22 us; the launch traced here: 21.9 us
  Pallas kernels  20.3 us (92%)
  local copies, waits for them, and re-layouts  1.57 us (7%)
    pallas_call x1, Pallas kernels, body(): pl.pallas_call(functools.partial(kernel, nx, ny, lx, ly, depth), out_shap...  20.3 us
    unnamed x1, local copies, waits for them, and re-layouts  1.57 us

profile of v2, /device:TPU:0, one launch (start us, length us, event | category | flops | bytes accessed | tf_op | source)
XLA Modules:
  0.0 21.9 jit_solution(6116236038984107618)
XLA Ops:
  0.0 20.3 %step.1 = f32[256,128]{1,0:T(8,128)} custom-call(f32[256,128]{1,0:T(8,128)} %bitcast.5, f32[256,128]{1,0:T(8,128)} %bitcast.6, f32[256,128]{1,0:T(8,128)} %bitcast.7), custom_call_target="tpu_custom_call" | custom-call | tf_op jit(solution)/shard_map/step/pallas_call | solution.py:349
  20.3 1.6 %copy.5 = f32[16,16,128]{2,1,0:T(8,128)} copy(f32[16,16,128]{2,1,0:T(8,128)} %bitcast.4) | data formatting | bytes 262144

commit v3 on v2

--- a/solution.py
+++ b/solution.py
@@ -348,7 +348,7 @@
         along_y = [vmem(ly, lx, depth)] * 4
         out = pl.pallas_call(
             functools.partial(kernel, nx, ny, lx, ly, depth),
-            out_shape=jax.ShapeDtypeStruct((lines, depth), f32),
+            out_shape=pltpu.VMEM((lines, depth), f32),
             in_specs=[pl.BlockSpec(memory_space=pltpu.HBM)] * 3,
             out_specs=pl.BlockSpec(memory_space=pltpu.VMEM),
             scratch_shapes=[vmem(lines, depth)] * 3 + along_x + along_y + [

time: 22 us -> 20.5 us (0.932)
  local copies, waits for them, and re-layouts: 1.57 us -> 0.66 us
  Pallas kernels: 20.3 us -> 19.7 us
    unnamed x1, local copies, waits for them, and re-layouts: 1.57 us -> 0.66 us
    pallas_call x1, Pallas kernels: 20.3 us -> 19.7 us  [body(): pl.pallas_call(functools.partial(kernel, nx, ny, lx, ly, depth), out_shap...]
where the time goes in v3:
time: 20.5 us; the launch traced here: 20.3 us
  Pallas kernels  19.7 us (96%)
  local copies, waits for them, and re-layouts  0.66 us (3%)
    pallas_call x1, Pallas kernels, body(): pl.pallas_call(functools.partial(kernel, nx, ny, lx, ly, depth), out_shap...  19.7 us
    unnamed x1, local copies, waits for them, and re-layouts  0.66 us

profile of v3, /device:TPU:0, one launch (start us, length us, event | category | flops | bytes accessed | tf_op | source)
XLA Modules:
  0.0 20.3 jit_solution(6443042161894308993)
XLA Ops:
  0.0 19.7 %step.1 = f32[256,128]{1,0:T(8,128)S(1)} custom-call(f32[256,128]{1,0:T(8,128)} %bitcast.5, f32[256,128]{1,0:T(8,128)} %bitcast.6, f32[256,128]{1,0:T(8,128)} %bitcast.7), custom_call_target="tpu_custom_call" | custom-call | tf_op jit(solution)/shard_map/step/pallas_call | solution.py:349
  19.7 0.7 %copy.5 = f32[16,16,128]{2,1,0:T(8,128)} copy(f32[16,16,128]{2,1,0:T(8,128)S(1)} %bitcast.4) | data formatting | bytes 262144

commit v4 on v3

--- a/solution.py
+++ b/solution.py
@@ -58,6 +58,7 @@
            pcr_lo, pcr_hi, pcr_inv, work, halo_out, halo_in,
            mat_x, mat_y, outer_x, inner_x, alpha_y, beta_y, own_y,
            part_x, part_y, out_y, mid_out, mid_in, chain_out, chain_in,
+           edge_in, part_e, pes_sem, per_sem,
            in_sem, hs_sem, hr_sem, mxs_sem, mxr_sem, mys_sem, myr_sem,
            pxs_sem, pxr_sem, pys_sem, pyr_sem, mid_sem):
     ix = lax.axis_index("gx")
@@ -163,33 +164,44 @@
                 - lo * (value - pltpu.roll(value, 1, 1)) - edge * value)
         work[row_x(i)] = 2.0 * (value + flux) + s_ref[row_x(i)]
 
+    value = f_ref[row_y(0)]
+    cond = c_ref[row_y(0)]
+    first_f, first_c = value, cond
+    flux_lo = None
+    for j in range(ly):
+        if j == ly - 1:
+            work[row_y(j)] += -flux_lo
+            break
+        next_f, next_c = f_ref[row_y(j + 1)], c_ref[row_y(j + 1)]
+        flux_hi = 0.5 * (cond + next_c) * (next_f - value)
+        work[row_y(j)] += flux_hi if flux_lo is None else flux_hi - flux_lo
+        value, cond, flux_lo = next_f, next_c, flux_hi
+
+    local = substitute([work[row_x(i)] for i in range(lx)],
+                       [None] + [mult_x[i] for i in range(1, lx)],
+                       [inv_x[i] for i in range(lx)])
+    part_x[rank, 0], part_x[rank, 1] = turn(local[0], local[-1])
+    parts_x = spread(lambda k: part_x.at[rank], part_x, rank, peer_x, half, pxs_sem, pxr_sem)
+    for i in range(lx):
+        work[row_x(i)] = local[i] - 2.0 * f_ref[row_x(i)]
+
     for copy in halos:
         copy.wait()
     below_f = jnp.where(iy == 0, 0.0, halo_in[1, 0])
     below_c = jnp.where(iy == 0, 0.0, halo_in[1, 1])
     above_f = jnp.where(iy == ny - 1, 0.0, halo_in[0, 0])
     above_c = jnp.where(iy == ny - 1, 0.0, halo_in[0, 1])
-    value = f_ref[row_y(0)]
-    cond = c_ref[row_y(0)]
-    flux_lo = 0.5 * (below_c + cond) * (value - below_f)
-    for j in range(ly):
-        if j == ly - 1:
-            next_f, next_c = above_f, above_c
-        else:
-            next_f, next_c = f_ref[row_y(j + 1)], c_ref[row_y(j + 1)]
-        flux_hi = 0.5 * (cond + next_c) * (next_f - value)
-        work[row_y(j)] += flux_hi - flux_lo
-        value, cond, flux_lo = next_f, next_c, flux_hi
-
-    local = substitute([work[row_x(i)] for i in range(lx)],
-                       [None] + [mult_x[i] for i in range(1, lx)],
-                       [inv_x[i] for i in range(lx)])
-    near, far = turn(local[0], local[-1])
-    part_x[rank, 0] = near
-    part_x[rank, 1] = far
-    parts_x = spread(lambda k: part_x.at[rank], part_x, rank, peer_x, half, pxs_sem, pxr_sem)
-    for i in range(lx):
-        work[row_x(i)] = local[i] - 2.0 * f_ref[row_x(i)]
+    edge_in[pl.ds(0, lx, stride=2)] = 0.5 * (below_c + first_c) * (below_f - first_f)
+    edge_in[pl.ds(1, lx, stride=2)] = 0.5 * (cond + above_c) * (above_f - value)
+    pair = pl.ds(0, 2, stride=ly - 1)
+    local = substitute([edge_in[pl.ds(2 * i, 2)] for i in range(lx)],
+                       [None] + [mult_x[i, pair] for i in range(1, lx)],
+                       [inv_x[i, pair] for i in range(lx)])
+    part_e[rank, 0], part_e[rank, 1] = turn(local[0], local[-1])
+    parts_e = spread(lambda k: part_e.at[rank], part_e, rank, peer_x, half, pes_sem, per_sem)
+    for i in range(lx):
+        rows = pl.ds(i * ly, 2, stride=ly - 1)
+        work[rows] = work[rows] + local[i]
 
     for i in range(lx):
         lo, hi, edge = faces_z(c_ref[row_x(i)])
@@ -210,7 +222,7 @@
 
     for copy in mats_x:
         copy.wait()
-    zeros = jnp.zeros_like(near)
+    zeros = jnp.zeros_like(mat_x[0, 2])
     outer_x[0, 0] = zeros
     outer_x[1, 0] = zeros
     outer_x[2, 0] = zeros
@@ -251,8 +263,12 @@
         own_y[1, k] = inverse
         joined = mat_y[k, 0] - mat_y[k, 1] * ratio
 
-    for copy in parts_x:
-        copy.wait()
+    for copy in parts_x + parts_e:
+        copy.wait()
+    for q in range(half):
+        for side in range(2):
+            part_x[q, side, pair] = part_x[q, side, pair] + part_e[q, side]
+    near, far = part_x[rank, 0], part_x[rank, 1]
     before = part_x[0, 1]
     for q in range(1, half):
         outer_x[2, q] = before
@@ -359,6 +375,7 @@
                 vmem(ny, lx, depth), vmem(ny, lx, depth), vmem(2, ny, lx, depth),
                 vmem(half, 2, ly, depth), vmem(ny, lx, depth), vmem(2, lx, depth),
                 vmem(2, ly, depth), vmem(2, ly, depth), vmem(ly, depth), vmem(ly, depth),
+                vmem(2 * lx, depth), vmem(half, 2, 2, depth), dma(half - 1), dma(half - 1),
                 dma(3), dma(2), dma(2), dma(half - 1), dma(half - 1), dma(ny - 1), dma(ny - 1),
                 dma(half - 1), dma(half - 1), dma(ny - 1), dma(ny - 1), dma(4),
             ],

time: 20.5 us -> 20.4 us (level)
  no operation moved by 1% of the time
where the time goes in v4:
time: 20.4 us; the launch traced here: 20.3 us
  Pallas kernels  19.6 us (96%)
  local copies, waits for them, and re-layouts  0.66 us (3%)
    pallas_call x1, Pallas kernels, body(): pl.pallas_call(functools.partial(kernel, nx, ny, lx, ly, depth), out_shap...  19.6 us
    unnamed x1, local copies, waits for them, and re-layouts  0.66 us

profile of v4, /device:TPU:0, one launch (start us, length us, event | category | flops | bytes accessed | tf_op | source)
XLA Modules:
  0.0 20.3 jit_solution(9367535422226439106)
XLA Ops:
  0.0 19.6 %step.1 = f32[256,128]{1,0:T(8,128)S(1)} custom-call(f32[256,128]{1,0:T(8,128)} %bitcast.5, f32[256,128]{1,0:T(8,128)} %bitcast.6, f32[256,128]{1,0:T(8,128)} %bitcast.7), custom_call_target="tpu_custom_call" | custom-call | tf_op jit(solution)/shard_map/step/pallas_call | solution.py:365
  19.6 0.7 %copy.5 = f32[16,16,128]{2,1,0:T(8,128)} copy(f32[16,16,128]{2,1,0:T(8,128)S(1)} %bitcast.4) | data formatting | bytes 262144

commit v5 on v4

--- a/solution.py
+++ b/solution.py
@@ -185,24 +185,6 @@
     for i in range(lx):
         work[row_x(i)] = local[i] - 2.0 * f_ref[row_x(i)]
 
-    for copy in halos:
-        copy.wait()
-    below_f = jnp.where(iy == 0, 0.0, halo_in[1, 0])
-    below_c = jnp.where(iy == 0, 0.0, halo_in[1, 1])
-    above_f = jnp.where(iy == ny - 1, 0.0, halo_in[0, 0])
-    above_c = jnp.where(iy == ny - 1, 0.0, halo_in[0, 1])
-    edge_in[pl.ds(0, lx, stride=2)] = 0.5 * (below_c + first_c) * (below_f - first_f)
-    edge_in[pl.ds(1, lx, stride=2)] = 0.5 * (cond + above_c) * (above_f - value)
-    pair = pl.ds(0, 2, stride=ly - 1)
-    local = substitute([edge_in[pl.ds(2 * i, 2)] for i in range(lx)],
-                       [None] + [mult_x[i, pair] for i in range(1, lx)],
-                       [inv_x[i, pair] for i in range(lx)])
-    part_e[rank, 0], part_e[rank, 1] = turn(local[0], local[-1])
-    parts_e = spread(lambda k: part_e.at[rank], part_e, rank, peer_x, half, pes_sem, per_sem)
-    for i in range(lx):
-        rows = pl.ds(i * ly, 2, stride=ly - 1)
-        work[rows] = work[rows] + local[i]
-
     for i in range(lx):
         lo, hi, edge = faces_z(c_ref[row_x(i)])
         excess = 1.0 + edge
@@ -219,6 +201,24 @@
             hi = b * pltpu.roll(hi, depth - shift, 1)
             shift, level = 2 * shift, level + 1
         pcr_inv[row_x(i)] = 1.0 / (excess + lo + hi)
+
+    for copy in halos:
+        copy.wait()
+    below_f = jnp.where(iy == 0, 0.0, halo_in[1, 0])
+    below_c = jnp.where(iy == 0, 0.0, halo_in[1, 1])
+    above_f = jnp.where(iy == ny - 1, 0.0, halo_in[0, 0])
+    above_c = jnp.where(iy == ny - 1, 0.0, halo_in[0, 1])
+    edge_in[pl.ds(0, lx, stride=2)] = 0.5 * (below_c + first_c) * (below_f - first_f)
+    edge_in[pl.ds(1, lx, stride=2)] = 0.5 * (cond + above_c) * (above_f - value)
+    pair = pl.ds(0, 2, stride=ly - 1)
+    local = substitute([edge_in[pl.ds(2 * i, 2)] for i in range(lx)],
+                       [None] + [mult_x[i, pair] for i in range(1, lx)],
+                       [inv_x[i, pair] for i in range(lx)])
+    part_e[rank, 0], part_e[rank, 1] = turn(local[0], local[-1])
+    parts_e = spread(lambda k: part_e.at[rank], part_e, rank, peer_x, half, pes_sem, per_sem)
+    for i in range(lx):
+        rows = pl.ds(i * ly, 2, stride=ly - 1)
+        work[rows] = work[rows] + local[i]
 
     for copy in mats_x:
         copy.wait()

time: 20.4 us -> 21.8 us (1.069)
  Pallas kernels: 19.6 us -> 21 us
    pallas_call x1, Pallas kernels: 19.6 us -> 21 us  [body(): pl.pallas_call(functools.partial(kernel, nx, ny, lx, ly, depth), out_shap...]
where the time goes in v5:
time: 21.8 us; the launch traced here: 21.7 us
  Pallas kernels  21 us (96%)
  local copies, waits for them, and re-layouts  0.66 us (3%)
    pallas_call x1, Pallas kernels, body(): pl.pallas_call(functools.partial(kernel, nx, ny, lx, ly, depth), out_shap...  21 us
    unnamed x1, local copies, waits for them, and re-layouts  0.66 us

profile of v5, /device:TPU:0, one launch (start us, length us, event | category | flops | bytes accessed | tf_op | source)
XLA Modules:
  0.0 21.7 jit_solution(12278972011123887329)
XLA Ops:
  0.0 21.0 %step.1 = f32[256,128]{1,0:T(8,128)S(1)} custom-call(f32[256,128]{1,0:T(8,128)} %bitcast.5, f32[256,128]{1,0:T(8,128)} %bitcast.6, f32[256,128]{1,0:T(8,128)} %bitcast.7), custom_call_target="tpu_custom_call" | custom-call | tf_op jit(solution)/shard_map/step/pallas_call | solution.py:365
  21.0 0.7 %copy.5 = f32[16,16,128]{2,1,0:T(8,128)} copy(f32[16,16,128]{2,1,0:T(8,128)S(1)} %bitcast.4) | data formatting | bytes 262144

commit v6 on v5

--- a/solution.py
+++ b/solution.py
@@ -156,6 +156,24 @@
         edge = jnp.where(low_end, 0.25 * cond, 0.0) + jnp.where(high_end, 0.25 * cond, 0.0)
         return lo, hi, edge
 
+    def factor_z(start, stop):
+        for i in range(start, stop):
+            lo, hi, edge = faces_z(c_ref[row_x(i)])
+            excess = 1.0 + edge
+            shift, level = 1, 0
+            while shift < depth:
+                inverse = 1.0 / (excess + lo + hi)
+                a = lo * pltpu.roll(inverse, shift, 1)
+                b = hi * pltpu.roll(inverse, depth - shift, 1)
+                pcr_lo[level, row_x(i)] = a
+                pcr_hi[level, row_x(i)] = b
+                excess = (excess + a * pltpu.roll(excess, shift, 1)
+                          + b * pltpu.roll(excess, depth - shift, 1))
+                lo = a * pltpu.roll(lo, shift, 1)
+                hi = b * pltpu.roll(hi, depth - shift, 1)
+                shift, level = 2 * shift, level + 1
+            pcr_inv[row_x(i)] = 1.0 / (excess + lo + hi)
+
     fetches[2].wait()
     for i in range(lx):
         value = f_ref[row_x(i)]
@@ -184,23 +202,6 @@
     parts_x = spread(lambda k: part_x.at[rank], part_x, rank, peer_x, half, pxs_sem, pxr_sem)
     for i in range(lx):
         work[row_x(i)] = local[i] - 2.0 * f_ref[row_x(i)]
-
-    for i in range(lx):
-        lo, hi, edge = faces_z(c_ref[row_x(i)])
-        excess = 1.0 + edge
-        shift, level = 1, 0
-        while shift < depth:
-            inverse = 1.0 / (excess + lo + hi)
-            a = lo * pltpu.roll(inverse, shift, 1)
-            b = hi * pltpu.roll(inverse, depth - shift, 1)
-            pcr_lo[level, row_x(i)] = a
-            pcr_hi[level, row_x(i)] = b
-            excess = (excess + a * pltpu.roll(excess, shift, 1)
-                      + b * pltpu.roll(excess, depth - shift, 1))
-            lo = a * pltpu.roll(lo, shift, 1)
-            hi = b * pltpu.roll(hi, depth - shift, 1)
-            shift, level = 2 * shift, level + 1
-        pcr_inv[row_x(i)] = 1.0 / (excess + lo + hi)
 
     for copy in halos:
         copy.wait()
@@ -219,6 +220,8 @@
     for i in range(lx):
         rows = pl.ds(i * ly, 2, stride=ly - 1)
         work[rows] = work[rows] + local[i]
+
+    factor_z(0, lx // 3)
 
     for copy in mats_x:
         copy.wait()
@@ -275,6 +278,7 @@
         before = part_x[q, 1] + ratios[q] * (before - part_x[q, 0])
     chain_out[...] = before
     chained = remote(chain_out, chain_in, mid_sem.at[2], mid_sem.at[3], mirror)
+    factor_z(lx // 3, 2 * lx // 3)
 
     mids.wait()
     joined = mid_in[0]
@@ -318,6 +322,7 @@
                     pys_sem, pyr_sem)
     for j in range(ly):
         work[row_y(j)] = local[j]
+    factor_z(2 * lx // 3, lx)
     scale = 1.0 / (1.0 - a * b)
     gain_in, gain_out = scale * own_y[0, iy], scale * own_y[1, iy]
     for copy in copies:

time: 21.8 us -> 18.3 us (0.84)
  Pallas kernels: 21 us -> 17.5 us
    pallas_call x1, Pallas kernels: 21 us -> 17.5 us  [body(): pl.pallas_call(functools.partial(kernel, nx, ny, lx, ly, depth), out_shap...]
where the time goes in v6:
time: 18.3 us; the launch traced here: 18.2 us
  Pallas kernels  17.5 us (96%)
  local copies, waits for them, and re-layouts  0.66 us (4%)
    pallas_call x1, Pallas kernels, body(): pl.pallas_call(functools.partial(kernel, nx, ny, lx, ly, depth), out_shap...  17.5 us
    unnamed x1, local copies, waits for them, and re-layouts  0.66 us

profile of v6, /device:TPU:0, one launch (start us, length us, event | category | flops | bytes accessed | tf_op | source)
XLA Modules:
  0.0 18.2 jit_solution(5496357418413060502)
XLA Ops:
  0.0 17.5 %step.1 = f32[256,128]{1,0:T(8,128)S(1)} custom-call(f32[256,128]{1,0:T(8,128)} %bitcast.5, f32[256,128]{1,0:T(8,128)} %bitcast.6, f32[256,128]{1,0:T(8,128)} %bitcast.7), custom_call_target="tpu_custom_call" | custom-call | tf_op jit(solution)/shard_map/step/pallas_call | solution.py:370
  17.5 0.7 %copy.5 = f32[16,16,128]{2,1,0:T(8,128)} copy(f32[16,16,128]{2,1,0:T(8,128)S(1)} %bitcast.4) | data formatting | bytes 262144
